TPU v7x, 128 devices: a whole 4x4x4 slice. The times are simulated.
128 devices in a mesh: outer: 16 (over z_lo, x, core), inner: 8 (over y, z_hi).
Axes of the slice: x: 4, y: 4, z: 4 (z_hi: 2, z_lo: 2; z = z_hi * 2 + z_lo), core: 2. Of those that a mesh axis runs over, the one named last changes fastest.
Arguments:
- hidden: bfloat16 [16384, 4096], P(('outer', 'inner')), may hold values from -16 to 16
- position: int32 [16384], P(('outer', 'inner')), may hold values from 0 to 16383, as said below
- query_weight: bfloat16 [4096, 512], replicated, may hold values from -0.09375 to 0.09375
- key_weight: bfloat16 [4096, 128], replicated, may hold values from -0.09375 to 0.09375
- value_weight: bfloat16 [4096, 128], replicated, may hold values from -0.09375 to 0.09375
- output_grad: bfloat16 [16384, 512], P(('outer', 'inner')), may hold values from -6 to 6
Outputs:
- attended: bfloat16 [16384, 512], P(('outer', 'inner'))
- hidden_grad: bfloat16 [16384, 4096], P(('outer', 'inner'))
- query_weight_grad: float32 [4096, 512], P(('outer', 'inner'))
- key_weight_grad: float32 [4096, 128], P(('outer', 'inner'))
- value_weight_grad: float32 [4096, 128], P(('outer', 'inner'))
Inputs may be any that keep to these rules, and one draw needn't show every extreme that they name: Each device's rows hold two runs of 64 consecutive positions in rising order: first the run that starts at a * 64, then the run that starts at (255 - a) * 64, for some a below 128 that differs from device to device; every position occurs once.
All inputs are finite; a program needn't handle non-finite values.
Results may differ from a plain program's by a relative error of at most 0.019.
The roundings to bfloat16 on the way count: a program that leaves them out, or rounds other values in their place, can miss the bound.
Values may be sent and summed in bfloat16 or wider, within the bound.
A program may use at most 128 MiB of HBM per device.

v0:
```python
import math

import jax
import jax.numpy as jnp
import numpy as np
from jax import lax
from jax.sharding import Mesh
from jax.sharding import PartitionSpec as P

HQ = 4
HD = 128
OUTER_INNER = ("outer_0", "outer_1", "outer_2", "inner_0", "inner_1")


rope_theta = 500000.0
masked_score = -1e30


def joined_along(pieces, dim):
    lengths = list(pieces.shape[1:])
    lengths[dim] *= pieces.shape[0]
    return jnp.moveaxis(pieces, 0, dim).reshape(lengths)


def one_gather(arrays, axis, dims):
    ravelled = jnp.concatenate([a.reshape(-1) for a in arrays])
    lines, at, done = (lax.all_gather(ravelled, axis), 0, [])
    for a, dim in zip(arrays, dims):
        pieces = lines[:, at : at + a.size].reshape(-1, *a.shape)
        done.append(joined_along(pieces, dim))
        at += a.size
    return tuple(done)


def in_blocks(shard, dim, size):
    before, after = (shard.shape[:dim], shard.shape[dim + 1 :])
    return jnp.moveaxis(shard.reshape(*before, size, -1, *after), dim, 0)


def piece_ends(length, count):
    unit = 8 if length >= 8 * count else 1
    return [length // unit * k // count * unit for k in range(1, count)]


def reduced_to_own(pieces, axes, order):
    lengths = [lax.axis_size(a) for a in axes]
    pieces = pieces.reshape(*lengths, *pieces.shape[1:])
    pieces = pieces.transpose(*order, *range(len(axes), pieces.ndim))
    pieces = pieces.reshape(-1, *pieces.shape[len(axes) :])
    for k in order:
        pieces = lax.psum_scatter(pieces, axes[k], scatter_dimension=0, tiled=True)
    return pieces[0]


def spread_scatter(shard, axes, dim):
    pieces = in_blocks(shard, dim, lax.axis_size(axes))
    cut = max(range(1, max(2, pieces.ndim - 1)), key=lambda d: pieces.shape[d])
    count, done = (len(axes), [])
    for leading, piece in enumerate(
        jnp.split(pieces, piece_ends(pieces.shape[cut], count), axis=cut)
    ):
        if piece.size:
            order = [(leading + k) % count for k in range(count)]
            done.append(reduced_to_own(piece, axes, order))
    return jnp.concatenate(done, axis=cut - 1)


def frequencies(head_width):
    exponents = np.arange(0, head_width, 2) / head_width
    plain_freq = rope_theta ** (-exponents)
    wavelength = 2.0 * np.pi / plain_freq
    blend = (8192.0 / wavelength - 1.0) / 3.0
    blended = (1.0 - blend) * plain_freq / 8.0 + blend * plain_freq
    scaled = np.where(
        wavelength > 8192.0, plain_freq / 8.0, np.where(wavelength < 2048.0, plain_freq, blended)
    )
    return jnp.asarray(scaled, dtype=jnp.float32)


def rope_tables(position):
    angles = position.astype(jnp.float32)[:, None] * frequencies(HD)[None, :]
    return (jnp.cos(angles), jnp.sin(angles))


def rotate(vector, cosine, sine_table):
    middle = vector.shape[-1] // 2
    leading = vector[..., :middle]
    trailing = vector[..., middle:]
    return jnp.concatenate(
        [leading * cosine - trailing * sine_table, trailing * cosine + leading * sine_table],
        axis=-1,
    )


def rotate_back(vector, cosine, sine_table):
    middle = vector.shape[-1] // 2
    leading = vector[..., :middle]
    trailing = vector[..., middle:]
    return jnp.concatenate(
        [leading * cosine + trailing * sine_table, trailing * cosine - leading * sine_table],
        axis=-1,
    )


def head_major(matrix, row_count):
    return matrix.reshape(row_count, HQ, HD).transpose(1, 0, 2).reshape(HQ * row_count, HD)


def pair_product(left, right):
    return lax.dot_general(
        left, right, (((1,), (1,)), ((), ())), preferred_element_type=jnp.float32
    )


def rows_product(left, right):
    return lax.dot_general(
        left, right, (((0,), (0,)), ((), ())), preferred_element_type=jnp.float32
    )


def block_scores(query_rows, query_pos, key_block, pos_block):
    scores = pair_product(query_rows, key_block) * float(HD) ** (-0.5)
    allowed = pos_block[None, :] <= query_pos[:, None]
    return (jnp.where(allowed, scores, masked_score), allowed)


def block_terms(
    query_rows, query_pos, grad_rows, log_total, row_delta, key_block, value_block, pos_block
):
    scores, allowed = block_scores(query_rows, query_pos, key_block, pos_block)
    probs_block = jnp.where(allowed, jnp.exp(scores - log_total[:, None]), 0.0)
    grad_probs = pair_product(grad_rows, value_block)
    grad_low = (probs_block * (grad_probs - row_delta[:, None])).astype(jnp.bfloat16)
    return (probs_block.astype(jnp.bfloat16), grad_low)


def key_value_rows(probs_low, grad_low, query_rows, grad_rows):
    key_part = rows_product(grad_low, query_rows) * float(HD) ** (-0.5)
    value_part = rows_product(probs_low, grad_rows)
    return jnp.concatenate([key_part, value_part], axis=1)


def slice_sources(sources, first_row, block_width):
    return tuple(
        (lax.dynamic_slice_in_dim(source, first_row, block_width, 0) for source in sources)
    )


def statistic_blocks(query_rows, query_pos, sources, block_count, block_width):
    query_total = query_rows.shape[0]

    def statistic_advance(block_index, running):
        row_max, row_sum = running
        key_block, value_block, pos_block = slice_sources(
            sources, block_index * block_width, block_width
        )
        scores, allowed = block_scores(query_rows, query_pos, key_block, pos_block)
        new_max = jnp.maximum(row_max, jnp.max(scores, axis=1))
        factor = jnp.exp(row_max - new_max)
        weights = jnp.where(allowed, jnp.exp(scores - new_max[:, None]), 0.0)
        row_sum = row_sum * factor + jnp.sum(weights, axis=1)
        return (new_max, row_sum)

    initial = (
        jnp.full((query_total,), masked_score, jnp.float32),
        jnp.zeros((query_total,), jnp.float32),
    )
    row_max, row_sum = lax.fori_loop(0, block_count, statistic_advance, initial)
    return row_max + jnp.log(row_sum)


def output_blocks(query_rows, query_pos, log_total, sources, block_count, block_width):

    def output_advance(block_index, weighted):
        key_block, value_block, pos_block = slice_sources(
            sources, block_index * block_width, block_width
        )
        scores, allowed = block_scores(query_rows, query_pos, key_block, pos_block)
        probs_block = jnp.where(allowed, jnp.exp(scores - log_total[:, None]), 0.0)
        return weighted + jnp.dot(
            probs_block.astype(jnp.bfloat16), value_block, preferred_element_type=jnp.float32
        )

    initial = jnp.zeros((query_rows.shape[0], HD), jnp.float32)
    return lax.fori_loop(0, block_count, output_advance, initial)


def backward_blocks(
    query_rows,
    query_pos,
    grad_rows,
    log_total,
    row_delta,
    sources,
    block_count,
    block_width,
    buffer,
):

    def backward_advance(block_index, carry):
        gathered, collected = carry
        first_row = block_index * block_width
        key_block, value_block, pos_block = slice_sources(sources, first_row, block_width)
        probs_low, grad_low = block_terms(
            query_rows,
            query_pos,
            grad_rows,
            log_total,
            row_delta,
            key_block,
            value_block,
            pos_block,
        )
        gathered = gathered + jnp.dot(grad_low, key_block, preferred_element_type=jnp.float32)
        rows = key_value_rows(probs_low, grad_low, query_rows, grad_rows)
        current = lax.dynamic_slice_in_dim(collected, first_row, block_width, 0)
        collected = lax.dynamic_update_slice_in_dim(collected, current + rows, first_row, 0)
        return (gathered, collected)

    initial = (jnp.zeros((query_rows.shape[0], HD), jnp.float32), buffer)
    gathered, collected = lax.fori_loop(0, block_count, backward_advance, initial)
    return (gathered * float(HD) ** (-0.5), collected)


def shards(hidden, position, query_weight, key_weight, value_weight, output_grad):
    row_count = hidden.shape[0]
    cosine, sine_table = rope_tables(position)
    query_proj = jnp.dot(hidden, query_weight, preferred_element_type=jnp.float32).reshape(
        row_count, HQ, HD
    )
    queries = rotate(query_proj, cosine[:, None, :], sine_table[:, None, :]).astype(jnp.bfloat16)
    key_rows = rotate(
        jnp.dot(hidden, key_weight, preferred_element_type=jnp.float32), cosine, sine_table
    ).astype(jnp.bfloat16)
    value_rows = jnp.dot(hidden, value_weight, preferred_element_type=jnp.float32).astype(
        jnp.bfloat16
    )
    key_all, value_all = one_gather((key_rows, value_rows), OUTER_INNER, (0, 0))
    pos_all = lax.all_gather(position, OUTER_INNER, axis=0, tiled=True)
    total_rows = key_all.shape[0]
    block_width = math.gcd(total_rows, 2048)
    query_rows = head_major(queries.reshape(row_count, HQ * HD), row_count)
    query_pos = jnp.tile(position, HQ)
    grad_rows = head_major(output_grad, row_count)
    stored_sources = (key_all, value_all, pos_all)
    log_total = statistic_blocks(
        query_rows, query_pos, stored_sources, total_rows // block_width, block_width
    )
    output = output_blocks(
        query_rows, query_pos, log_total, stored_sources, total_rows // block_width, block_width
    )
    attended = (
        output.reshape(HQ, row_count, HD)
        .transpose(1, 0, 2)
        .reshape(row_count, HQ * HD)
        .astype(jnp.bfloat16)
    )
    row_delta = jnp.sum(grad_rows.astype(jnp.float32) * output, axis=1)
    empty = jnp.zeros((total_rows, 2 * HD), jnp.float32)
    grad_heads, collected = backward_blocks(
        query_rows,
        query_pos,
        grad_rows,
        log_total,
        row_delta,
        stored_sources,
        total_rows // block_width,
        block_width,
        empty,
    )
    key_value_sum = lax.psum_scatter(collected, OUTER_INNER, scatter_dimension=0, tiled=True)
    grad_tokens = grad_heads.reshape(HQ, row_count, HD).transpose(1, 0, 2)
    grad_query = (
        rotate_back(grad_tokens, cosine[:, None, :], sine_table[:, None, :])
        .reshape(row_count, HQ * HD)
        .astype(jnp.bfloat16)
    )
    grad_key = rotate_back(key_value_sum[:, :HD], cosine, sine_table).astype(jnp.bfloat16)
    grad_value = key_value_sum[:, HD:].astype(jnp.bfloat16)
    hidden_grad = pair_product(grad_query, query_weight)
    hidden_grad = hidden_grad + pair_product(grad_key, key_weight)
    hidden_grad = hidden_grad + pair_product(grad_value, value_weight)
    hidden_grad = hidden_grad.astype(jnp.bfloat16)
    grad_all = jnp.concatenate([grad_query, grad_key, grad_value], axis=1)
    weight_sum = spread_scatter(rows_product(hidden, grad_all), OUTER_INNER, 0)
    query_width = HQ * HD
    query_weight_grad = weight_sum[:, :query_width]
    key_weight_grad = weight_sum[:, query_width : query_width + HD]
    value_weight_grad = weight_sum[:, query_width + HD :]
    return (attended, hidden_grad, query_weight_grad, key_weight_grad, value_weight_grad)


def solution(mesh):
    split = Mesh(
        mesh.devices.reshape(2, 4, 2, 4, 2), ("outer_0", "outer_1", "outer_2", "inner_0", "inner_1")
    )
    placed = (P(OUTER_INNER, None), P(OUTER_INNER), P(), P(), P(), P(OUTER_INNER, None))
    return jax.shard_map(
        shards,
        mesh=split,
        in_specs=placed,
        out_specs=(
            P(OUTER_INNER, None),
            P(OUTER_INNER, None),
            P(OUTER_INNER, None),
            P(OUTER_INNER, None),
            P(OUTER_INNER, None),
        ),
        check_vma=False,
    )
```

profile of v0, /device:TPU:0, one launch (start us, length us, event | category | flops | bytes accessed | tf_op | source)
XLA Modules:
  0.0 1841.4 jit_solution(2304850106631633285)
XLA Ops:
  16.7 318.6 %all-gather.1 = s32[128,1,128]{2,1,0:T(1,128)S(1)} all-gather(s32[1,1,128]{2,1,0:T(1,128)S(1)} %bitcast.150), channel_id=1, replica_groups=mesh['outer_0'=2,'outer_1'=4,'outer_2'=2,'inner_0'=4,'inner_1'=2] {'oute..., dimensions={0}, use_global_device_ids=true | all-gather | bytes 66048 | tf_op jit(solution)/shard_map/all_gather | solution.py:239
  369.3 26.1 %while.46 = (s32[]{:T(128)}, f32[512]{0:T(512)S(1)}, f32[512]{0:T(512)S(1)}, s32[16384]{0:T(1024)S(1)}, bf16[16384,128]{1,0:T(8,128)(2,1)}, /*index=5*/bf16[512,...) while((s32[]{:T(128)}, f32[512]{0:T(512)S(1)}, ...), condition=%wide.region_3.4_spmd.clone, body=%wide.region_0.3_spmd.clone.sunk | while | flops 278923776 | bytes 9110198 | solution.py:168
  395.5 25.8 %while.47 = (s32[]{:T(128)}, f32[512,128]{1,0:T(8,128)S(1)}, s32[16384]{0:T(1024)S(1)}, bf16[16384,128]{1,0:T(8,128)(2,1)}, bf16[512,128]{1,0:T(8,128)(2,1)S(1)}...) while((s32[]{:T(128)}, f32[512,128]{1,0:T(8,128)S(1)}, ...), condition=%wide.region_5.6_spmd.clone, body=%wide.region_4.5_spmd.clone.sunk | while | flops 543293440 | bytes 1736888 | solution.py:185
  429.2 86.8 %while.48 = (s32[]{:T(128)}, f32[512,128]{1,0:T(8,128)S(1)}, f32[16384,256]{0,1:T(8,128)}, s32[16384]{0:T(1024)S(1)}, bf16[16384,128]{1,0:T(8,128)(2,1)}, /*inde...) while((s32[]{:T(128)}, f32[512,128]{1,0:T(8,128)S(1)}, ...), condition=%wide.region_8.9_spmd.clone, body=%wide.region_7.8_spmd.clone.sunk | while | flops 1353056256 | bytes 29917920 | solution.py:221
  517.0 683.6 %reduce-scatter.27.cloned.1.call-done = f32[128,256]{0,1:T(8,128)} async-done(((f32[16384,256]{0,1:T(8,128)}), f32[128,256]{0,1:T(8,128)}) %reduce-scatter.27.cloned.1.call-update) | async-done | bytes 131088 | tf_op jit(solution)/shard_map/reduce_scatter | solution.py:271
  1250.0 15.1 reduce-scatter.39.cloned.1.call-done
  1265.2 40.3 %reduce-scatter.59.cloned.1.call-done = f32[32,6,768]{2,1,0:T(8,128)} async-done(((f32[128,6,768]{2,1,0:T(8,128)}), f32[32,6,768]{2,1,0:T(8,128)}) %reduce-scatter.59.cloned.1.call-update) | async-done | bytes 589840 | tf_op jit(solution)/shard_map/reduce_scatter | solution.py:51
  1305.5 47.9 %reduce-scatter.29.cloned.1.call-done = f32[64,6,768]{2,1,0:T(8,128)} async-done(((f32[128,6,768]{2,1,0:T(8,128)}), f32[64,6,768]{2,1,0:T(8,128)}) %reduce-scatter.29.cloned.1.call-update) | async-done | bytes 1179664 | tf_op jit(solution)/shard_map/reduce_scatter | solution.py:51
  1353.5 17.1 reduce-scatter.49.cloned.1.call-done
  1370.7 51.3 %reduce-scatter.69.cloned.1.call-done = f32[64,7,768]{2,1,0:T(8,128)} async-done(((f32[128,7,768]{2,1,0:T(8,128)}), f32[64,7,768]{2,1,0:T(8,128)}) %reduce-scatter.69.cloned.1.call-update) | async-done | bytes 1376272 | tf_op jit(solution)/shard_map/reduce_scatter | solution.py:51
  1434.4 25.4 %reduce-scatter.61.cloned.1.call-done = f32[16,6,768]{2,1,0:T(8,128)} async-done(((f32[32,6,768]{2,1,0:T(8,128)}), f32[16,6,768]{2,1,0:T(8,128)}) %reduce-scatter.61.cloned.1.call-update) | async-done | bytes 294928 | tf_op jit(solution)/shard_map/reduce_scatter | solution.py:51
  1459.8 27.0 %reduce-scatter.31.cloned.1.call-done = f32[16,6,768]{2,1,0:T(8,128)} async-done(((f32[64,6,768]{2,1,0:T(8,128)}), f32[16,6,768]{2,1,0:T(8,128)}) %reduce-scatter.31.cloned.1.call-update) | async-done | bytes 294928 | tf_op jit(solution)/shard_map/reduce_scatter | solution.py:51
  1486.9 27.9 %reduce-scatter.51.cloned.1.call-done = f32[16,7,768]{2,1,0:T(8,128)} async-done(((f32[64,7,768]{2,1,0:T(8,128)}), f32[16,7,768]{2,1,0:T(8,128)}) %reduce-scatter.51.cloned.1.call-update) | async-done | bytes 344080 | tf_op jit(solution)/shard_map/reduce_scatter | solution.py:51
  1514.9 30.6 %reduce-scatter.71.cloned.1.call-done = f32[32,7,768]{2,1,0:T(8,128)} async-done(((f32[64,7,768]{2,1,0:T(8,128)}), f32[32,7,768]{2,1,0:T(8,128)}) %reduce-scatter.71.cloned.1.call-update) | async-done | bytes 688144 | tf_op jit(solution)/shard_map/reduce_scatter | solution.py:51
  1545.6 24.6 %reduce-scatter.43.cloned.1.call-done = f32[4,6,768]{2,1,0:T(8,128)} async-done(((f32[16,6,768]{2,1,0:T(8,128)}), f32[4,6,768]{2,1,0:T(8,128)}) %reduce-scatter.43.cloned.1.call-update) | async-done | bytes 73744 | tf_op jit(solution)/shard_map/reduce_scatter | solution.py:51
  1570.2 17.7 reduce-scatter.63.cloned.1.call-done
  1601.5 21.0 %reduce-scatter.53.cloned.1.call-done = f32[8,7,768]{2,1,0:T(8,128)} async-done(((f32[16,7,768]{2,1,0:T(8,128)}), f32[8,7,768]{2,1,0:T(8,128)}) %reduce-scatter.53.cloned.1.call-update) | async-done | bytes 172048 | tf_op jit(solution)/shard_map/reduce_scatter | solution.py:51
  1622.6 24.0 %reduce-scatter.73.cloned.1.call-done = f32[8,7,768]{2,1,0:T(8,128)} async-done(((f32[32,7,768]{2,1,0:T(8,128)}), f32[8,7,768]{2,1,0:T(8,128)}) %reduce-scatter.73.cloned.1.call-update) | async-done | bytes 172048 | tf_op jit(solution)/shard_map/reduce_scatter | solution.py:51
  1646.7 16.2 reduce-scatter.45.cloned.1.call-done
  1662.9 22.2 %reduce-scatter.65.cloned.1.call-done = f32[2,6,768]{2,1,0:T(8,128)} async-done(((f32[8,6,768]{2,1,0:T(8,128)}), f32[2,6,768]{2,1,0:T(8,128)}) %reduce-scatter.65.cloned.1.call-update) | async-done | bytes 36880 | tf_op jit(solution)/shard_map/reduce_scatter | solution.py:51
  1685.2 22.6 %reduce-scatter.35.cloned.1.call-done = f32[2,6,768]{2,1,0:T(8,128)} async-done(((f32[8,6,768]{2,1,0:T(8,128)}), f32[2,6,768]{2,1,0:T(8,128)}) %reduce-scatter.35.cloned.1.call-update) | async-done | bytes 36880 | tf_op jit(solution)/shard_map/reduce_scatter | solution.py:51
  1766.7 18.0 reduce-scatter.37.cloned.1.call-done
  1784.7 22.0 %reduce-scatter.57.cloned.1.call-done = f32[1,7,768]{2,1,0:T(8,128)} async-done(((f32[4,7,768]{2,1,0:T(8,128)}), f32[1,7,768]{2,1,0:T(8,128)}) %reduce-scatter.57.cloned.1.call-update) | async-done | bytes 21520 | tf_op jit(solution)/shard_map/reduce_scatter | solution.py:51
  1806.7 22.6 %reduce-scatter.77.cloned.1.call-done = f32[1,7,768]{2,1,0:T(8,128)} async-done(((f32[4,7,768]{2,1,0:T(8,128)}), f32[1,7,768]{2,1,0:T(8,128)}) %reduce-scatter.77.cloned.1.call-update) | async-done | bytes 21520 | tf_op jit(solution)/shard_map/reduce_scatter | solution.py:51
  (267 shorter events, 329.8 us)
Async XLA Ops:
  7.2 328.1 %all-gather.4.cloned.1.call-start = ((), (), s32[]{:S(2)}) async-start(), calls=%async_computation.52 | async-start | bytes 8454144 | tf_op jit(solution)/shard_map/all_gather | solution.py:27
  12.9 1187.7 %reduce-scatter.27.cloned.1.call-start = ((), (), s32[]{:S(2)}) async-start(), calls=%async_computation.26 | async-start | bytes 16908288 | tf_op jit(solution)/shard_map/reduce_scatter | solution.py:271
  516.0 749.1 %reduce-scatter.39.cloned.1.call-start = ((), (), s32[]{:S(2)}) async-start(), calls=%async_computation.32 | async-start | bytes 3932160 | tf_op jit(solution)/shard_map/reduce_scatter | solution.py:51
  1237.1 116.3 %reduce-scatter.29.cloned.1.call-start = ((), (), s32[]{:S(2)}) async-start(), calls=%async_computation.27 | async-start | bytes 4718592 | tf_op jit(solution)/shard_map/reduce_scatter | solution.py:51
  1237.7 132.9 %reduce-scatter.49.cloned.1.call-start = ((), (), s32[]{:S(2)}) async-start(), calls=%async_computation.37 | async-start | bytes 4718592 | tf_op jit(solution)/shard_map/reduce_scatter | solution.py:51
  1245.8 176.2 %reduce-scatter.69.cloned.1.call-start = ((), (), s32[]{:S(2)}) async-start(), calls=%async_computation.47 | async-start | bytes 4718592 | tf_op jit(solution)/shard_map/reduce_scatter | solution.py:51
  1249.9 184.3 %reduce-scatter.41.cloned.1.call-start = ((), (), s32[]{:S(2)}) async-start(), calls=%async_computation.33 | async-start | bytes 1179648 | tf_op jit(solution)/shard_map/reduce_scatter | solution.py:51
  1265.1 194.6 %reduce-scatter.61.cloned.1.call-start = ((), (), s32[]{:S(2)}) async-start(), calls=%async_computation.43 | async-start | bytes 1179648 | tf_op jit(solution)/shard_map/reduce_scatter | solution.py:51
  1305.5 181.3 %reduce-scatter.31.cloned.1.call-start = ((), (), s32[]{:S(2)}) async-start(), calls=%async_computation.28 | async-start | bytes 1966080 | tf_op jit(solution)/shard_map/reduce_scatter | solution.py:51
  1353.4 161.4 %reduce-scatter.51.cloned.1.call-start = ((), (), s32[]{:S(2)}) async-start(), calls=%async_computation.38 | async-start | bytes 1966080 | tf_op jit(solution)/shard_map/reduce_scatter | solution.py:51
  1370.6 174.9 %reduce-scatter.71.cloned.1.call-start = ((), (), s32[]{:S(2)}) async-start(), calls=%async_computation.48 | async-start | bytes 2359296 | tf_op jit(solution)/shard_map/reduce_scatter | solution.py:51
  1422.0 148.2 %reduce-scatter.43.cloned.1.call-start = ((), (), s32[]{:S(2)}) async-start(), calls=%async_computation.34 | async-start | bytes 491520 | tf_op jit(solution)/shard_map/reduce_scatter | solution.py:51
  1434.3 153.6 %reduce-scatter.63.cloned.1.call-start = ((), (), s32[]{:S(2)}) async-start(), calls=%async_computation.44 | async-start | bytes 589824 | tf_op jit(solution)/shard_map/reduce_scatter | solution.py:51
  1459.8 141.6 %reduce-scatter.33.cloned.1.call-start = ((), (), s32[]{:S(2)}) async-start(), calls=%async_computation.29 | async-start | bytes 589824 | tf_op jit(solution)/shard_map/reduce_scatter | solution.py:51
  1486.8 135.7 %reduce-scatter.53.cloned.1.call-start = ((), (), s32[]{:S(2)}) async-start(), calls=%async_computation.39 | async-start | bytes 589824 | tf_op jit(solution)/shard_map/reduce_scatter | solution.py:51
  1514.8 131.8 %reduce-scatter.73.cloned.1.call-start = ((), (), s32[]{:S(2)}) async-start(), calls=%async_computation.49 | async-start | bytes 983040 | tf_op jit(solution)/shard_map/reduce_scatter | solution.py:51
  1545.5 117.3 %reduce-scatter.45.cloned.1.call-start = ((), (), s32[]{:S(2)}) async-start(), calls=%async_computation.35 | async-start | bytes 147456 | tf_op jit(solution)/shard_map/reduce_scatter | solution.py:51
  1570.2 115.0 %reduce-scatter.65.cloned.1.call-start = ((), (), s32[]{:S(2)}) async-start(), calls=%async_computation.45 | async-start | bytes 245760 | tf_op jit(solution)/shard_map/reduce_scatter | solution.py:51
  1587.9 120.0 %reduce-scatter.35.cloned.1.call-start = ((), (), s32[]{:S(2)}) async-start(), calls=%async_computation.30 | async-start | bytes 245760 | tf_op jit(solution)/shard_map/reduce_scatter | solution.py:51
  1601.4 122.1 %reduce-scatter.55.cloned.1.call-start = ((), (), s32[]{:S(2)}) async-start(), calls=%async_computation.40 | async-start | bytes 294912 | tf_op jit(solution)/shard_map/reduce_scatter | solution.py:51
  1622.6 114.5 %reduce-scatter.75.cloned.1.call-start = ((), (), s32[]{:S(2)}) async-start(), calls=%async_computation.50 | async-start | bytes 294912 | tf_op jit(solution)/shard_map/reduce_scatter | solution.py:51
  1646.7 106.8 %reduce-scatter.47.cloned.1.call-start = ((), (), s32[]{:S(2)}) async-start(), calls=%async_computation.36 | async-start | bytes 73728 | tf_op jit(solution)/shard_map/reduce_scatter | solution.py:51
  1662.9 103.8 %reduce-scatter.67.cloned.1.call-start = ((), (), s32[]{:S(2)}) async-start(), calls=%async_computation.46 | async-start | bytes 73728 | tf_op jit(solution)/shard_map/reduce_scatter | solution.py:51
  1723.6 105.7 %reduce-scatter.77.cloned.1.call-start = ((), (), s32[]{:S(2)}) async-start(), calls=%async_computation.51 | async-start | bytes 122880 | tf_op jit(solution)/shard_map/reduce_scatter | solution.py:51
  (8 other events, 630.4 us)
Sparse Core Ops, SparseCore 0:
  13.0 313.9 all-gather.3
  516.1 684.4 reduce-scatter.26
  1233.1 31.9 reduce-scatter.38
  1267.4 38.0 reduce-scatter.58
  1307.6 45.7 reduce-scatter.28
  1355.6 14.9 reduce-scatter.48
  1372.9 48.9 reduce-scatter.68
  1436.6 23.0 reduce-scatter.60
  1462.0 24.7 reduce-scatter.30
  1489.2 25.5 reduce-scatter.50
  1517.0 28.4 reduce-scatter.70
  1547.9 22.2 reduce-scatter.42
  1572.3 15.4 reduce-scatter.62
  1590.1 11.2 reduce-scatter.32
  1603.6 18.8 reduce-scatter.52
  1624.8 21.8 reduce-scatter.72
  1648.8 14.0 reduce-scatter.44
  1665.2 19.8 reduce-scatter.64
  1687.4 20.4 reduce-scatter.34
  1710.2 13.3 reduce-scatter.54
  1739.4 14.0 reduce-scatter.46
  1769.0 15.6 reduce-scatter.36
  1786.9 19.7 reduce-scatter.56
  1808.9 20.3 reduce-scatter.76
  (3 shorter events, 31.9 us)
where the time goes:
time: 1840 us
  waiting for transfers between devices  1250 us (68%)
  blocking collectives  319 us (17%)
  matrix products  124 us (7%)
  local copies, waits for them, and re-layouts  90.3 us (5%)
  other arithmetic  40 us (2%)
    reduce_scatter x1, waiting for transfers between devices, shards(): lax.psum_scatter(collected, OUTER_INNER, scatter_dimension=0, tiled=True)  684 us
    reduce_scatter x25, waiting for transfers between devices, reduced_to_own(): pieces = lax.psum_scatter(pieces, axes[k], scatter_dimension=0, tiled=True)  567 us
    all_gather x1, blocking collectives, shards(): pos_all = lax.all_gather(position, OUTER_INNER, axis=0, tiled=True)  319 us
    dot_general x27, matrix products, pair_product(): lax.dot_general(left, right, (((1,), (1,)), ((), ())), preferred_element_...  57.9 us
  transfers between devices with their start and end apart: 27, of which 26 were waited for; matrix products, arithmetic and copies ran while one was open for 2% of the time, Pallas kernels for 0%

commit v1 on v0

v1 whole, which is shorter than its diff:
```python
import functools
import math

import jax
import jax.numpy as jnp
import numpy as np
from jax import lax
from jax.experimental import pallas as pl
from jax.experimental.pallas import tpu as pltpu
from jax.sharding import Mesh
from jax.sharding import PartitionSpec as P

HQ = 4
HD = 128
TOK = 128
CHIPS = 64
AXES = ("zl", "x", "c", "y", "zh")
ORDERS = (("x", "y", "z"), ("y", "z", "x"), ("z", "x", "y"))
MESH = pl.DeviceIdType.MESH
rope_theta = 500000.0
masked_score = -1e30
SCALE = float(HD) ** -0.5
LOG2E = math.log2(math.e)
VMEM_LIMIT = 64 * 1024 * 1024 - 131072
F32 = jnp.float32
BF16 = jnp.bfloat16


def frequencies(head_width):
    exponents = np.arange(0, head_width, 2) / head_width
    plain_freq = rope_theta ** (-exponents)
    wavelength = 2.0 * np.pi / plain_freq
    blend = (8192.0 / wavelength - 1.0) / 3.0
    blended = (1.0 - blend) * plain_freq / 8.0 + blend * plain_freq
    scaled = np.where(
        wavelength > 8192.0, plain_freq / 8.0, np.where(wavelength < 2048.0, plain_freq, blended)
    )
    return jnp.asarray(scaled, dtype=jnp.float32)


def here():
    zl, zh = lax.axis_index("zl"), lax.axis_index("zh")
    return {"x": lax.axis_index("x"), "y": lax.axis_index("y"), "z": zh * 2 + zl}


def along(axis, value):
    if axis == "z":
        return {"zl": value % 2, "zh": value // 2}
    return {axis: value}


def place(fixed):
    whole = slice(None)
    z = fixed.get("z")
    return (
        whole if z is None else z % 2,
        fixed.get("x", whole),
        fixed.get("y", whole),
        whole if z is None else z // 2,
    )


def left_dims(fixed):
    dims = []
    for name, size in (("z", 2), ("x", 4), ("y", 4), ("z", 2)):
        if name not in fixed:
            dims.append(size)
    return tuple(dims)


def enter(me, ring=True, partner=True):
    barrier = pltpu.get_barrier_semaphore()
    count = 0
    if ring:
        for axis in "xyz":
            for delta in (1, 3):
                pl.semaphore_signal(
                    barrier, inc=1, device_id=along(axis, (me[axis] + delta) % 4), device_id_type=MESH
                )
                count += 1
    if partner:
        pl.semaphore_signal(
            barrier, inc=1, device_id={"c": 1 - lax.axis_index("c")}, device_id_type=MESH
        )
        count += 1
    pl.semaphore_wait(barrier, count)


def remote(src, dst, sems, device_id):
    return pltpu.make_async_remote_copy(
        src_ref=src,
        dst_ref=dst,
        send_sem=sems[0],
        recv_sem=sems[1],
        device_id=device_id,
        device_id_type=MESH,
    )


def params(collective_id=None):
    if collective_id is None:
        return pltpu.CompilerParams(vmem_limit_bytes=VMEM_LIMIT)
    return pltpu.CompilerParams(
        collective_id=collective_id, has_side_effects=True, vmem_limit_bytes=VMEM_LIMIT
    )


def in_vmem(n):
    return [pl.BlockSpec(memory_space=pltpu.VMEM)] * n


KV_ROWS = TOK + 16
PART = KV_ROWS // 3


class Spread:
    def __init__(self, me, axis, spot, first, ref, send, recv, waits):
        self.me, self.axis, self.spot, self.first, self.ref = me, axis, spot, first, ref
        self.send, self.recv, self.waits = send, recv, waits

    def hop(self, slot, src, dst, delta):
        copy = remote(
            src,
            dst,
            (self.send.at[slot], self.recv.at[slot]),
            along(self.axis, (self.me[self.axis] + delta) % 4),
        )
        copy.start()
        self.waits.append(copy)
        return copy

    def start(self):
        dst = self.ref.at[self.spot(self.me[self.axis], slice(None))]
        src = dst if self.first is None else self.first
        self.near = (self.hop(0, src, dst, 1), self.hop(1, src, dst, 3))

    def forward(self):
        self.far = []
        for half, delta, origin in ((0, 1, 3), (1, 3, 1)):
            self.near[half].wait_recv()
            ref = self.ref.at[self.spot((self.me[self.axis] + origin) % 4, half)]
            self.far.append(self.hop(2 + half, ref, ref, delta))

    def finish(self):
        for copy in self.far:
            copy.wait_recv()


def gather_kernel(
    kv, q, do, tables, hid, kv_all, q_pair, do_pair, tables_pair, meta_pair, hid_partner,
    send, recv, pair_send, pair_recv,
):
    me = here()
    core = lax.axis_index("c")
    other = {"c": 1 - core}
    enter(me)
    pair, waits = [], []

    def to_partner(src, dst):
        n = len(pair)
        copy = remote(src, dst, (pair_send.at[n], pair_recv.at[n]), other)
        copy.start()
        pair.append(copy)

    def spread(k, ring, axis, fixed, first=None):
        rows = pl.ds(PART * k, PART)

        def spot(value, half):
            return (*place({**fixed, axis: value}), half, rows)

        return Spread(me, axis, spot, first, kv_all, send.at[k, ring], recv.at[k, ring], waits)

    lines, planes, spaces = [], [], []
    for k, (a, b, c) in enumerate(ORDERS):
        rows = pl.ds(PART * k, PART)
        lines.append(spread(k, 0, a, {b: me[b], c: me[c]}, kv.at[:, rows]))
        planes.append(spread(k, 1, b, {c: me[c]}))
        spaces.append(
            [spread(k, 2 + n, c, {b: (me[b] + off) % 4}) for n, off in enumerate((0, 3, 1, 2))]
        )

    for k in range(3):
        lines[k].start()
    kv_all[place(me)] = kv[...]
    to_partner(q, q_pair.at[core])
    to_partner(do, do_pair.at[core])
    to_partner(tables, tables_pair.at[core])
    to_partner(kv.at[0, pl.ds(TOK, 16)], meta_pair.at[core])
    for g in range(8):
        at = pl.multiple_of((2 * g + 1 - core) * 256, 256)
        to_partner(hid.at[:, pl.ds(at, 256)], hid_partner.at[:, pl.ds(g * 256, 256)])
    q_pair[core] = q[...]
    do_pair[core] = do[...]
    tables_pair[core] = tables[...]
    meta_pair[core] = kv[0, TOK : TOK + 16]
    for k in range(3):
        lines[k].forward()
    for k in range(3):
        lines[k].finish()
        planes[k].start()
        spaces[k][0].start()
    for k in range(3):
        planes[k].forward()
        spaces[k][1].start()
        spaces[k][2].start()
    for k in range(3):
        spaces[k][0].forward()
    for k in range(3):
        planes[k].finish()
        spaces[k][3].start()
    for n in range(1, 4):
        for k in range(3):
            spaces[k][n].forward()
    for n in range(4):
        for k in range(3):
            spaces[k][n].finish()
    for copy in waits:
        copy.wait_send()
    for copy in pair:
        copy.wait()


def gather(kv, q, do, tables, hid):
    n_pair = 12
    return pl.pallas_call(
        gather_kernel,
        out_shape=(
            jax.ShapeDtypeStruct((2, 4, 4, 2, 2, KV_ROWS, HD), BF16),
            jax.ShapeDtypeStruct((2, *q.shape), BF16),
            jax.ShapeDtypeStruct((2, *do.shape), BF16),
            jax.ShapeDtypeStruct((2, *tables.shape), F32),
            jax.ShapeDtypeStruct((2, 16, HD), BF16),
            jax.ShapeDtypeStruct((TOK, 2048), BF16),
        ),
        in_specs=[*in_vmem(4), pl.BlockSpec(memory_space=pl.ANY)],
        out_specs=(*in_vmem(5), pl.BlockSpec(memory_space=pl.ANY)),
        scratch_shapes=[
            pltpu.SemaphoreType.DMA((3, 6, 4)),
            pltpu.SemaphoreType.DMA((3, 6, 4)),
            pltpu.SemaphoreType.DMA((n_pair,)),
            pltpu.SemaphoreType.DMA((n_pair,)),
        ],
        compiler_params=params(0),
        name="gather_kv",
    )(kv, q, do, tables, hid)


def unit_loop(fixed, body):
    dims = left_dims(fixed)
    count = math.prod(dims)
    if count == 1:
        body(())
        return

    def step(i, carry):
        index, rest = [], i
        for size in reversed(dims):
            index.append(rest % size)
            rest = rest // size
        body(tuple(reversed(index)))
        return carry

    lax.fori_loop(0, count, step, 0)


def ring_slots(tails):
    shapes = []
    for (a, b, c), tail in zip(ORDERS, tails):
        dims = left_dims((a, b))
        shapes.append(pltpu.VMEM((4, 6, *dims, *tail), BF16))
        shapes.append(pltpu.VMEM((6, *dims, *tail), BF16))
        shapes.append(pltpu.VMEM((6, *tail), BF16))
    return shapes


class Collect:
    def __init__(self, me, axis, fixed, x, subs, buf, send, recv, waits):
        self.me, self.axis, self.fixed, self.x, self.subs = me, axis, fixed, x, subs
        self.buf, self.send, self.recv, self.waits = buf, send, recv, waits
        self.copies = {}

    def chunks(self, delta, half):
        value = (self.me[self.axis] + delta) % 4
        return self.x.at[(*place({**self.fixed, self.axis: value}), *self.subs(half))]

    def post(self, message, bound, half, delta):
        copy = remote(
            self.chunks(bound, half),
            self.buf.at[message],
            (self.send.at[message], self.recv.at[message]),
            along(self.axis, (self.me[self.axis] + delta) % 4),
        )
        copy.start()
        self.waits.append(copy)
        self.copies[message] = copy

    def start_far(self):
        self.post(0, 2, 0, 1)
        self.post(3, 2, 1, 3)

    def start_right(self):
        self.post(1, 1, 1, 1)

    def start_left(self):
        self.post(4, 3, 0, 3)

    def start(self):
        self.start_far()
        self.start_right()
        self.start_left()

    def add(self, delta, half, messages, finish=None):
        for message in messages:
            self.copies[message].wait_recv()
        ref = self.chunks(delta, half)
        buf = self.buf

        def body(index):
            whole = (*index, slice(None), slice(None))
            total = ref[whole].astype(F32)
            for message in messages:
                total = total + buf[(message, *whole)].astype(F32)
            if finish is None:
                ref[whole] = total.astype(BF16)
            else:
                finish(half, total)

        unit_loop({**self.fixed, self.axis: 0}, body)

    def forward(self):
        self.add(1, 0, (0,))
        self.post(2, 1, 0, 1)
        self.add(3, 1, (3,))
        self.post(5, 3, 1, 3)

    def collect(self, finish=None):
        self.add(0, 1, (1, 5), finish)
        self.add(0, 0, (4, 2), finish)


def reduce_to_own(me, x, slots, subs, send, recv, finish, meanwhile=None):
    waits = []
    first, second, third = [], [], []
    for k, (a, b, c) in enumerate(ORDERS):
        mine = functools.partial(subs, k)
        one, two, three = slots[3 * k : 3 * k + 3]
        first.append(
            [
                Collect(
                    me, a, {b: (me[b] + off) % 4}, x, mine, one.at[n], send.at[k, n], recv.at[k, n], waits
                )
                for n, off in enumerate((2, 1, 3, 0))
            ]
        )
        second.append(Collect(me, b, {a: me[a]}, x, mine, two, send.at[k, 4], recv.at[k, 4], waits))
        third.append(
            Collect(me, c, {a: me[a], b: me[b]}, x, mine, three, send.at[k, 5], recv.at[k, 5], waits)
        )
    colours = range(3)
    for n in range(2):
        for k in colours:
            first[k][n].start()
    if meanwhile is not None:
        meanwhile()
    for k in colours:
        first[k][0].forward()
    for k in colours:
        first[k][2].start()
    for k in colours:
        first[k][1].forward()
    for k in colours:
        first[k][3].start()
    for k in colours:
        first[k][0].collect()
        second[k].start_far()
    for k in colours:
        first[k][2].forward()
    for k in colours:
        first[k][1].collect()
        second[k].start_right()
    for k in colours:
        first[k][3].forward()
    for k in colours:
        first[k][2].collect()
        second[k].start_left()
    for k in colours:
        second[k].forward()
    for k in colours:
        first[k][3].collect()
    for k in colours:
        second[k].collect()
        third[k].start()
    for k in colours:
        third[k].forward()
    for k in colours:
        third[k].collect(functools.partial(finish, k))
    for copy in waits:
        copy.wait_send()


DKV_PARTS = ((0, 48), (48, 48), (96, 32))


def scatter_kv_kernel(
    part, dq, dq_pair, dkv_pair, x, dq_in, *rest
):
    slots, (send, recv, pair_send, pair_recv, load_sem) = rest[:9], rest[9:]
    me = here()
    core = lax.axis_index("c")
    other = {"c": 1 - core}
    load = pltpu.make_async_copy(part, x, load_sem)
    load.start()
    enter(me)
    load.wait()
    first = remote(dq.at[1 - core], dq_in, (pair_send.at[0], pair_recv.at[0]), other)
    first.start()

    def subs(k, half):
        return (half, pl.ds(*DKV_PARTS[k]), slice(None))

    def finish(k, half, value):
        dkv_pair[(core, half, pl.ds(*DKV_PARTS[k]))] = value

    second = remote(
        dq_pair.at[core], dq_pair.at[core], (pair_send.at[1], pair_recv.at[1]), other
    )

    def meanwhile():
        first.wait()
        dq_pair[core] = dq[core] + dq_in[...]
        second.start()

    reduce_to_own(me, x, slots, subs, send, recv, finish, meanwhile)
    third = remote(
        dkv_pair.at[core], dkv_pair.at[core], (pair_send.at[2], pair_recv.at[2]), other
    )
    third.start()
    second.wait()
    third.wait()


def scatter_kv(part, dq):
    return pl.pallas_call(
        scatter_kv_kernel,
        out_shape=(
            jax.ShapeDtypeStruct(dq.shape, F32),
            jax.ShapeDtypeStruct((2, 2, TOK, HD), F32),
        ),
        in_specs=[pl.BlockSpec(memory_space=pl.ANY), *in_vmem(1)],
        out_specs=tuple(in_vmem(2)),
        scratch_shapes=[
            pltpu.VMEM(part.shape, BF16),
            pltpu.VMEM(dq.shape[1:], F32),
            *ring_slots([(n, HD) for _, n in DKV_PARTS]),
            pltpu.SemaphoreType.DMA((3, 6, 6)),
            pltpu.SemaphoreType.DMA((3, 6, 6)),
            pltpu.SemaphoreType.DMA((3,)),
            pltpu.SemaphoreType.DMA((3,)),
            pltpu.SemaphoreType.DMA,
        ],
        compiler_params=params(2),
        name="scatter_kv",
    )(part, dq)


def scatter_weights_kernel(part, out, x, *rest):
    slots, (send, recv, load_sem) = rest[:9], rest[9:]
    me = here()
    load = pltpu.make_async_copy(part, x, load_sem)
    load.start()
    enter(me, partner=False)
    load.wait()

    def columns(k, half):
        return pl.ds((2 * k + half) * 128, 128)

    def subs(k, half):
        return (slice(None), columns(k, half))

    def finish(k, half, value):
        out[(slice(None), columns(k, half))] = value

    reduce_to_own(me, x, slots, subs, send, recv, finish)


def scatter_weights(part):
    return pl.pallas_call(
        scatter_weights_kernel,
        out_shape=jax.ShapeDtypeStruct(part.shape[4:], F32),
        in_specs=[pl.BlockSpec(memory_space=pl.ANY)],
        out_specs=in_vmem(1)[0],
        scratch_shapes=[
            pltpu.VMEM(part.shape, BF16),
            *ring_slots([(32, 128)] * 3),
            pltpu.SemaphoreType.DMA((3, 6, 6)),
            pltpu.SemaphoreType.DMA((3, 6, 6)),
            pltpu.SemaphoreType.DMA,
        ],
        compiler_params=params(3),
        name="scatter_weights",
    )(part)


def swap_kernel(a, b, a_in, b_in, send, recv):
    other = {"c": 1 - lax.axis_index("c")}
    enter(None, ring=False)
    one = remote(a, a_in, (send.at[0], recv.at[0]), other)
    two = remote(b, b_in, (send.at[1], recv.at[1]), other)
    one.start()
    two.start()
    one.wait()
    two.wait()


def swap(a, b):
    return pl.pallas_call(
        swap_kernel,
        out_shape=(jax.ShapeDtypeStruct(a.shape, a.dtype), jax.ShapeDtypeStruct(b.shape, b.dtype)),
        in_specs=in_vmem(2),
        out_specs=tuple(in_vmem(2)),
        scratch_shapes=[pltpu.SemaphoreType.DMA((2,)), pltpu.SemaphoreType.DMA((2,))],
        compiler_params=params(1),
        name="swap_partials",
    )(a, b)


KEYS = 256
CHUNKS = 16


def dot_nt(a, b):
    return lax.dot_general(a, b, (((1,), (1,)), ((), ())), preferred_element_type=F32)


def dot_nn(a, b):
    return lax.dot_general(a, b, (((1,), (0,)), ((), ())), preferred_element_type=F32)


def dot_tn(a, b):
    return lax.dot_general(a, b, (((0,), (0,)), ((), ())), preferred_element_type=F32)


def by_run(dst, src, d):
    for run in range(2):
        for h in range(HQ):
            dst[run, d, h * 64 : (h + 1) * 64, :] = src[
                d, run * 64 : (run + 1) * 64, h * HD : (h + 1) * HD
            ]


def edge_of(table, d):
    return jnp.minimum(table[128 + d] // 4, CHUNKS - 1)


def aside(edge, j):
    sel = (j >= edge).astype(jnp.int32)
    return sel, j + sel


def run_start(a, sel):
    return (a if sel == 0 else 255 - a) * 64


def chunk(ref, *index):
    return ref[(*index[:-1], pl.ds(4 * index[-1], 4))].reshape(KEYS, HD)


def forward_kernel(
    table, kv, q, ks, vs, o, lse, dense_scores, edge_scores, qs, top, total
):
    def put(b, carry):
        r = table[b]
        ks[0, r] = kv[b, 0, 0:64]
        ks[1, r] = kv[b, 0, 64:128]
        vs[0, r] = kv[b, 1, 0:64]
        vs[1, r] = kv[b, 1, 64:128]
        return carry

    lax.fori_loop(0, CHIPS, put, 0, unroll=4)
    for d in range(2):
        by_run(qs, q, d)
    top[...] = jnp.full_like(top, -1e29)
    total[...] = jnp.zeros_like(total)
    o[...] = jnp.zeros_like(o)

    lane = lax.broadcasted_iota(jnp.int32, (1, KEYS), 1)
    row = lax.broadcasted_iota(jnp.int32, (256, KEYS), 0) % 64
    edges = [edge_of(table, d) for d in range(2)]

    def dense(it, carry):
        s = dot_nt(qs[1].reshape(512, HD), chunk(ks, 0, it))
        dense_scores[it] = s
        top[1] = jnp.maximum(top[1], jnp.maximum(s[:, :HD], s[:, HD:]).reshape(2, 256, HD))
        return carry

    def plain(j, carry):
        for d in range(2):
            sel, ch = aside(edges[d], j)
            s = dot_nt(qs[sel, d], chunk(ks, sel, ch))
            edge_scores[d, j] = s
            top[sel, d] = jnp.maximum(top[sel, d], jnp.maximum(s[:, :HD], s[:, HD:]))
        return carry

    lax.fori_loop(0, CHUNKS, dense, 0, unroll=2)
    lax.fori_loop(0, CHUNKS - 1, plain, 0, unroll=3)
    for d in range(2):
        for sel in range(2):
            s = dot_nt(qs[sel, d], chunk(ks, sel, edges[d]))
            own = run_start(table[130 + d], sel)
            starts = [run_start(table[64 + 4 * edges[d] + r], sel) - own for r in range(4)]
            offset = jnp.where(
                lane < 128,
                jnp.where(lane < 64, starts[0], starts[1]),
                jnp.where(lane < 192, starts[2], starts[3]),
            ) + lane % 64
            s = jnp.where(offset <= row, s, masked_score)
            edge_scores[d, CHUNKS - 1 + sel] = s
            top[sel, d] = jnp.maximum(top[sel, d], jnp.maximum(s[:, :HD], s[:, HD:]))

    factor = SCALE * LOG2E
    for d in range(2):
        for sel in range(2):
            peak = jnp.max(top[sel, d], axis=1, keepdims=True)
            top[sel, d] = jnp.broadcast_to(peak * factor, (256, HD))

    def weights(s, peak):
        p0 = jnp.exp2(s[:, :HD] * factor - peak)
        p1 = jnp.exp2(s[:, HD:] * factor - peak)
        return p0 + p1, jnp.concatenate([p0.astype(BF16), p1.astype(BF16)], axis=1)

    def dense_out(it, carry):
        both, p = weights(dense_scores[it], top[1].reshape(512, HD))
        total[1] += both.reshape(2, 256, HD)
        o[1] += dot_nn(p, chunk(vs, 0, it)).reshape(2, 256, HD)
        return carry

    def edge_out(d, j, sel, ch):
        both, p = weights(edge_scores[d, j], top[sel, d])
        total[sel, d] += both
        o[sel, d] += dot_nn(p, chunk(vs, sel, ch))

    def plain_out(j, carry):
        for d in range(2):
            edge_out(d, j, *aside(edges[d], j))
        return carry

    lax.fori_loop(0, CHUNKS, dense_out, 0, unroll=2)
    lax.fori_loop(0, CHUNKS - 1, plain_out, 0, unroll=3)
    for d in range(2):
        for sel in range(2):
            edge_out(d, CHUNKS - 1 + sel, sel, edges[d])

    for d in range(2):
        for sel in range(2):
            summed = jnp.sum(total[sel, d], axis=1, keepdims=True)
            some = summed > 0.0
            safe = jnp.where(some, summed, 1.0)
            o[sel, d] = o[sel, d] / safe
            level = top[sel, d] * (1.0 / LOG2E) + jnp.log(safe)
            lse[sel, d] = jnp.where(some, level, masked_score)


def forward(table, kv, q):
    sorted_shape = jax.ShapeDtypeStruct((2, CHIPS, 64, HD), BF16)
    rows = jax.ShapeDtypeStruct((2, 2, 256, HD), F32)
    return pl.pallas_call(
        forward_kernel,
        out_shape=(sorted_shape, sorted_shape, rows, rows),
        in_specs=[pl.BlockSpec(memory_space=pltpu.SMEM), *in_vmem(2)],
        out_specs=tuple(in_vmem(4)),
        scratch_shapes=[
            pltpu.VMEM((CHUNKS, 512, KEYS), F32),
            pltpu.VMEM((2, CHUNKS + 1, 256, KEYS), F32),
            pltpu.VMEM((2, 2, 256, HD), BF16),
            pltpu.VMEM((2, 2, 256, HD), F32),
            pltpu.VMEM((2, 2, 256, HD), F32),
        ],
        compiler_params=params(),
        name="attention_forward",
    )(table, kv, q)


def backward_kernel(
    table, ks, vs, q, do, o, lse, o_in, lse_in,
    attended, part, dq,
    qs, dos, level, delta, final, grads, dqs,
):
    for d in range(2):
        by_run(qs, q, d)
        by_run(dos, do, d)
        for sel in range(2):
            one, two = lse[sel, d], lse_in[sel, d]
            most = jnp.maximum(one, two)
            w1, w2 = jnp.exp(one - most), jnp.exp(two - most)
            both = w1 + w2
            out = (o[sel, d] * w1 + o_in[sel, d] * w2) / both
            final[sel, d] = out
            logs = (most + jnp.log(both)) * LOG2E
            level[sel, d] = jnp.transpose(logs)[0:8]
            dots = jnp.sum(dos[sel, d].astype(F32) * out, axis=1, keepdims=True)
            delta[sel, d] = jnp.transpose(jnp.broadcast_to(dots, (256, HD)))[0:8]
    core = table[132]
    for run in range(2):
        for h in range(HQ):
            attended[run * 64 : (run + 1) * 64, h * HD : (h + 1) * HD] = final[
                run, core, h * 64 : (h + 1) * 64, :
            ].astype(BF16)

    dqs[...] = jnp.zeros_like(dqs)

    def clear(i, carry):
        for sel in range(2):
            for which in range(2):
                grads[sel, which, i] = jnp.zeros((64, HD), F32)
        return carry

    lax.fori_loop(0, CHIPS, clear, 0, unroll=4)

    factor = SCALE * LOG2E
    edges = [edge_of(table, d) for d in range(2)]

    def terms(k, v, qq, gg, lev, dl, mask=None):
        p = jnp.exp2(dot_nt(k, qq) * factor - lev)
        if mask is not None:
            p = mask(p)
        ds = p * (dot_nt(v, gg) - dl)
        return p.astype(BF16), ds.astype(BF16)

    def collect(ksel, ch, p, ds, qq, gg):
        spot = pl.ds(4 * ch, 4)
        grads[ksel, 0, spot] += dot_nn(ds, qq).reshape(4, 64, HD)
        grads[ksel, 1, spot] += dot_nn(p, gg).reshape(4, 64, HD)

    def dense(it, carry):
        k, v = chunk(ks, 0, it), chunk(vs, 0, it)
        qq, gg = qs[1].reshape(512, HD), dos[1].reshape(512, HD)
        lev = jnp.concatenate([level[1, 0, 0:1], level[1, 1, 0:1]], axis=1)
        dl = jnp.concatenate([delta[1, 0, 0:1], delta[1, 1, 0:1]], axis=1)
        p, ds = terms(k, v, qq, gg, lev, dl)
        collect(0, it, p, ds, qq, gg)
        dqs[1] += dot_tn(ds, k).reshape(2, 256, HD)
        return carry

    def one(d, sel, ch, mask=None):
        k, v = chunk(ks, sel, ch), chunk(vs, sel, ch)
        qq, gg = qs[sel, d], dos[sel, d]
        p, ds = terms(k, v, qq, gg, level[sel, d, 0:1], delta[sel, d, 0:1], mask)
        return sel, ch, k, qq, gg, p, ds

    def gather_in(d, sel, ch, k, qq, gg, p, ds):
        collect(sel, ch, p, ds, qq, gg)
        dqs[sel, d] += dot_tn(ds, k)

    def plain(j, carry):
        found = [one(d, *aside(edges[d], j)) for d in range(2)]
        for d in range(2):
            gather_in(d, *found[d])
        return carry

    lax.fori_loop(0, CHUNKS, dense, 0, unroll=2)
    lax.fori_loop(0, CHUNKS - 1, plain, 0, unroll=3)

    difference = (
        lax.broadcasted_iota(jnp.int32, (64, 256), 1) % 64
        - lax.broadcasted_iota(jnp.int32, (64, 256), 0)
    )
    for d in range(2):
        for sel in range(2):
            own = run_start(table[130 + d], sel)

            def mask(p, d=d, sel=sel, own=own):
                pieces = []
                for r in range(4):
                    least = run_start(table[64 + 4 * edges[d] + r], sel) - own
                    pieces.append(
                        jnp.where(difference >= least, p[64 * r : 64 * (r + 1)], 0.0)
                    )
                return jnp.concatenate(pieces, axis=0)

            gather_in(d, *one(d, sel, edges[d], mask))

    for d in range(2):
        for sel in range(2):
            dq[d, sel] = dqs[sel, d] * SCALE

    def put(b, carry):
        r = table[b]
        for sel in range(2):
            part[b, 0, 64 * sel : 64 * (sel + 1)] = (grads[sel, 0, r] * SCALE).astype(BF16)
            part[b, 1, 64 * sel : 64 * (sel + 1)] = grads[sel, 1, r].astype(BF16)
        return carry

    lax.fori_loop(0, CHIPS, put, 0, unroll=4)


def backward(table, ks, vs, q, do, o, lse, o_in, lse_in):
    return pl.pallas_call(
        backward_kernel,
        out_shape=(
            jax.ShapeDtypeStruct((TOK, HQ * HD), BF16),
            jax.ShapeDtypeStruct((CHIPS, 2, TOK, HD), BF16),
            jax.ShapeDtypeStruct((2, 2, 256, HD), F32),
        ),
        in_specs=[pl.BlockSpec(memory_space=pltpu.SMEM), *in_vmem(8)],
        out_specs=tuple(in_vmem(3)),
        scratch_shapes=[
            pltpu.VMEM((2, 2, 256, HD), BF16),
            pltpu.VMEM((2, 2, 256, HD), BF16),
            pltpu.VMEM((2, 2, 8, 256), F32),
            pltpu.VMEM((2, 2, 8, 256), F32),
            pltpu.VMEM((2, 2, 256, HD), F32),
            pltpu.VMEM((2, 2, CHIPS, 64, HD), F32),
            pltpu.VMEM((2, 2, 256, HD), F32),
        ],
        compiler_params=params(),
        name="attention_backward",
    )(table, ks, vs, q, do, o, lse, o_in, lse_in)


def turned(u, cosine, sine):
    return u * cosine + pltpu.roll(u, 64, 1) * sine


def tail_kernel(
    table, dq, dkv, tables, hidden, hid_in, wq, wk, wv,
    hidden_grad, part,
    grads, hid, wq_in, wk_in, wv_in, sems,
):
    core = table[132]
    loads = []

    def load(src, dst):
        copy = pltpu.make_async_copy(src, dst, sems.at[len(loads)])
        copy.start()
        loads.append(copy)

    for g in range(8):
        at = pl.multiple_of((2 * g + core) * 256, 256)
        load(hidden.at[:, pl.ds(at, 256)], hid.at[pl.ds(0, TOK), pl.ds(g * 256, 256)])
    load(hid_in, hid.at[pl.ds(TOK, TOK)])
    load(wq, wq_in)
    load(wk, wk_in)
    load(wv, wv_in)

    for n in range(2):
        d = core if n == 0 else 1 - core
        base = n * TOK
        for run in range(2):
            rows = slice(run * 64, (run + 1) * 64)
            cosine, sine = tables[d, 0, rows], tables[d, 1, rows]
            for h in range(HQ):
                g = turned(dq[d, run, h * 64 : (h + 1) * 64], cosine, sine)
                grads[base + run * 64 : base + (run + 1) * 64, h * HD : (h + 1) * HD] = g.astype(BF16)
        gk = turned(dkv[d, 0], tables[d, 0], tables[d, 1])
        grads[base : base + TOK, 512:640] = gk.astype(BF16)
        grads[base : base + TOK, 640:768] = dkv[d, 1].astype(BF16)

    for copy in loads[:9]:
        copy.wait()
    for g in range(8):
        block = dot_tn(hid[:, g * 256 : (g + 1) * 256], grads[...])
        part[g // 4, g % 4] = block.astype(BF16).reshape(4, 2, 32, 768)
    for copy in loads[9:]:
        copy.wait()

    def columns(n, carry):
        rows = pl.ds(pl.multiple_of(n * 256, 256), 256)
        both = jnp.concatenate([wk_in[rows], wv_in[rows]], axis=1)
        block = dot_nt(grads[0:TOK, 0:512], wq_in[rows]) + dot_nt(grads[0:TOK, 512:768], both)
        hidden_grad[:, rows] = block.astype(BF16)
        return carry

    lax.fori_loop(0, 16, columns, 0, unroll=2)


def tail(table, dq, dkv, tables, hidden, hid_in, wq, wk, wv):
    return pl.pallas_call(
        tail_kernel,
        out_shape=(
            jax.ShapeDtypeStruct((TOK, 4096), BF16),
            jax.ShapeDtypeStruct((2, 4, 4, 2, 32, 768), BF16),
        ),
        in_specs=[
            pl.BlockSpec(memory_space=pltpu.SMEM),
            *in_vmem(3),
            *[pl.BlockSpec(memory_space=pl.ANY)] * 5,
        ],
        out_specs=tuple(in_vmem(2)),
        scratch_shapes=[
            pltpu.VMEM((2 * TOK, 768), BF16),
            pltpu.VMEM((2 * TOK, 2048), BF16),
            pltpu.VMEM(wq.shape, BF16),
            pltpu.VMEM(wk.shape, BF16),
            pltpu.VMEM(wv.shape, BF16),
            pltpu.SemaphoreType.DMA((12,)),
        ],
        compiler_params=params(),
        name="token_grads",
    )(table, dq, dkv, tables, hidden, hid_in, wq, wk, wv)


def project_kernel(
    first, hidden, tables, wq, wk, wv, kv, q, acc, hid, wq_in, wk_in, wv_in, sems
):
    copies = []
    for n in range(4):
        rows = pl.ds(n * 1024, 1024)
        group = []
        for src, dst in (
            (hidden.at[:, rows], hid.at[:, rows]),
            (wq.at[rows], wq_in.at[rows]),
            (wk.at[rows], wk_in.at[rows]),
            (wv.at[rows], wv_in.at[rows]),
        ):
            copy = pltpu.make_async_copy(src, dst, sems.at[n, len(group)])
            copy.start()
            group.append(copy)
        copies.append(group)
    for n in range(4):
        for copy in copies[n]:
            copy.wait()
        rows = slice(n * 1024, (n + 1) * 1024)
        h = hid[:, rows]
        both = jnp.concatenate([wk_in[rows], wv_in[rows]], axis=1)
        left, right = dot_nn(h, wq_in[rows]), dot_nn(h, both)
        if n == 0:
            acc[:, :512] = left
            acc[:, 512:] = right
        else:
            acc[:, :512] += left
            acc[:, 512:] += right
    cosine, sine = tables[0], tables[1]

    def rotated(u):
        return (u * cosine - pltpu.roll(u, 64, 1) * sine).astype(BF16)

    for h in range(HQ):
        q[:, h * HD : (h + 1) * HD] = rotated(acc[:, h * HD : (h + 1) * HD])
    kv[0, 0:TOK] = rotated(acc[:, 512:640])
    kv[1, 0:TOK] = acc[:, 640:768].astype(BF16)
    index = (first[0] // 64).astype(F32)
    for n in range(2):
        kv[n, TOK:KV_ROWS] = jnp.full((16, HD), index, F32).astype(BF16)


def project(first, hidden, tables, wq, wk, wv):
    anywhere = pl.BlockSpec(memory_space=pl.ANY)
    return pl.pallas_call(
        project_kernel,
        out_shape=(
            jax.ShapeDtypeStruct((2, KV_ROWS, HD), BF16),
            jax.ShapeDtypeStruct((TOK, HQ * HD), BF16),
        ),
        in_specs=[
            pl.BlockSpec(memory_space=pltpu.SMEM), anywhere, *in_vmem(1), anywhere, anywhere, anywhere
        ],
        out_specs=tuple(in_vmem(2)),
        scratch_shapes=[
            pltpu.VMEM((TOK, 768), F32),
            pltpu.VMEM(hidden.shape, BF16),
            pltpu.VMEM(wq.shape, BF16),
            pltpu.VMEM(wk.shape, BF16),
            pltpu.VMEM(wv.shape, BF16),
            pltpu.SemaphoreType.DMA((4, 4)),
        ],
        compiler_params=params(),
        name="project",
    )(first, hidden, tables, wq, wk, wv)


def shards(hidden, position, query_weight, key_weight, value_weight, output_grad):
    core = lax.axis_index("c")
    angles = position.astype(F32)[:, None] * frequencies(HD)[None, :]
    cosine, sine = jnp.cos(angles), jnp.sin(angles)
    cos2 = jnp.concatenate([cosine, cosine], axis=1)
    sin2 = jnp.concatenate([sine, -sine], axis=1)
    tables = jnp.stack([cos2, sin2])

    kv, q = project(position[:1], hidden, tables, query_weight, key_weight, value_weight)
    kv_all, q_pair, do_pair, tables_pair, meta_pair, hid_in = gather(
        kv, q, output_grad, tables, hidden
    )
    kv_all = kv_all.reshape(CHIPS, 2, KV_ROWS, HD)
    runs = kv_all[:, 0, TOK, 0].astype(jnp.int32)
    below = (runs[None, :] < runs[:, None]).astype(jnp.int32)
    rank = jnp.sum(below, axis=1)
    slots = lax.iota(jnp.int32, CHIPS)
    rising = jnp.sum(jnp.where(rank[None, :] == slots[:, None], runs[None, :], 0), axis=1)
    own = meta_pair[:, 0, 0].astype(jnp.int32)
    count = jnp.sum((runs[None, :] < own[:, None]).astype(jnp.int32), axis=1)
    table = jnp.concatenate(
        [rank, rising, count, own, core[None].astype(jnp.int32), jnp.zeros((3,), jnp.int32)]
    )

    ks, vs, o, lse = forward(table, kv_all, q_pair)
    o_in, lse_in = swap(o, lse)
    attended, part, dq = backward(table, ks, vs, q_pair, do_pair, o, lse, o_in, lse_in)
    dq_pair, dkv_pair = scatter_kv(part.reshape(2, 4, 4, 2, 2, TOK, HD), dq)
    hidden_grad, weights = tail(
        table, dq_pair, dkv_pair, tables_pair, hidden, hid_in, query_weight, key_weight, value_weight
    )
    total = scatter_weights(weights)
    return attended, hidden_grad, total[:, :512], total[:, 512:640], total[:, 640:]


def solution(mesh):
    split = Mesh(mesh.devices.reshape(2, 4, 2, 4, 2), AXES)
    rows = P(AXES, None)
    return jax.shard_map(
        shards,
        mesh=split,
        in_specs=(rows, P(AXES), P(), P(), P(), rows),
        out_specs=(rows,) * 5,
        check_vma=False,
    )
```

time: 1840 us -> 172 us (0.09)
  waiting for transfers between devices: 1250 us -> 0 us
  blocking collectives: 319 us -> 0 us
  Pallas kernels: 0 us -> 162 us
  matrix products: 124 us -> 0 us
  local copies, waits for them, and re-layouts: 90.3 us -> 3.48 us
  other arithmetic: 40 us -> 5.8 us
    reduce_scatter x26 -> x0, waiting for transfers between devices: 1250 us -> none  [the longest x1 684 us: shards(): lax.psum_scatter(collected, OUTER_INNER, scatter_dimension=0, tiled=True)]
    all_gather x1 -> x0, blocking collectives: 319 us -> none  [shards(): pos_all = lax.all_gather(position, OUTER_INNER, axis=0, tiled=True)]
    pallas_call x0 -> x8, Pallas kernels: none -> 162 us  [the longest x1 41.1 us: gather(): pl.pallas_call(gather_kernel, out_shape=(jax.ShapeDtypeStruct((2, 4, 4, 2...]
    dot_general x63 -> x0, matrix products: 124 us -> none  [the longest x27 57.9 us: pair_product(): lax.dot_general(left, right, (((1,), (1,)), ((), ())), preferred_element_...]
    dynamic_update_slice x8 -> x0, other arithmetic: 26 us -> none  [backward_advance(): lax.dynamic_update_slice_in_dim(collected, current + rows, first_row, 0)]
  transfers between devices with their start and end apart: 27 -> 0, of which waited for: 26 -> 0; matrix products, arithmetic and copies ran while one was open for 2% -> 0% of each run, Pallas kernels for 0% -> 0%
where the time goes in v1:
time: 172 us
  Pallas kernels  162 us (94%)
  other arithmetic  5.8 us (3%)
  local copies, waits for them, and re-layouts  3.48 us (2%)
    pallas_call x1, Pallas kernels, gather(): pl.pallas_call(gather_kernel, out_shape=(jax.ShapeDtypeStruct((2, 4, 4, 2...  41.1 us
    pallas_call x1, Pallas kernels, scatter_kv(): pl.pallas_call(scatter_kv_kernel, out_shape=(jax.ShapeDtypeStruct(dq.shap...  34.5 us
    pallas_call x1, Pallas kernels, scatter_weights(): pl.pallas_call(scatter_weights_kernel, out_shape=jax.ShapeDtypeStruct(par...  27.7 us
    pallas_call x1, Pallas kernels, backward(): pl.pallas_call(backward_kernel, out_shape=(jax.ShapeDtypeStruct((TOK, HQ...  22.6 us
    pallas_call x1, Pallas kernels, forward(): pl.pallas_call(forward_kernel, out_shape=(sorted_shape, sorted_shape, row...  15.5 us
    pallas_call x1, Pallas kernels, tail(): pl.pallas_call(tail_kernel, out_shape=(jax.ShapeDtypeStruct((TOK, 4096),...  9.48 us
    pallas_call x1, Pallas kernels, project(): pl.pallas_call(project_kernel, out_shape=(jax.ShapeDtypeStruct((2, KV_ROW...  5.9 us
    pallas_call x1, Pallas kernels, swap(): pl.pallas_call(swap_kernel, out_shape=(jax.ShapeDtypeStruct(a.shape, a.dt...  4.9 us

profile of v1, /device:TPU:0, one launch (start us, length us, event | category | flops | bytes accessed | tf_op | source)
XLA Modules:
  0.0 171.7 jit_solution(8491294508649417953)
XLA Ops:
  0.6 0.7 convert_element_type.33
  1.3 1.0 multiply_cosine_fusion
  2.3 0.1 maximum_bitcast_fusion
  2.4 0.7 pad_maximum_fusion.tables
  3.0 5.9 %project.1 = (bf16[2,144,128]{2,1,0:T(8,128)(2,1)}, bf16[128,512]{1,0:T(8,128)(2,1)}) custom-call(s32[1]{0:T(128)} %bitcast.11, bf16[128,4096]{1,0:T(8,128)(2,1)} %hidden.3, f32[2,128,128]{2,1,0:T(8,128)} %pad_maximum_fusion.tables, bf16[4096,512]{1,0:T(8,128)(2,1)} %wq.3, bf16[4096,128]{1,0:T(8,128)(2,1)} %wk.3, bf16[4096,128]{1,0:T(8,128)(2,1)} %wv.3), custom_call_target="tpu_custom_call" | custom-call | tf_op jit(solution)/shard_map/project/pallas_call | solution.py:948
  8.9 41.1 %gather_kv.1 = (bf16[2,4,4,2,2,144,128]{6,5,4,3,2,1,0:T(8,128)(2,1)}, bf16[2,128,512]{2,1,0:T(8,128)(2,1)}, bf16[2,128,512]{2,1,0:T(8,128)(2,1)}, f32[2,2,128,12...) custom-call(bf16[2,144,128]{2,1,0:T(8,128)(2,1)} %get-tuple-element.26.kv, ...), custom_call_target="tpu_custom_call" | custom-call | tf_op jit(solution)/shard_map/gather_kv/pallas_call | solution.py:225
  50.0 2.1 %fusion = s32[64]{0:T(128)S(1)} fusion(bf16[64,2,144,128]{3,2,1,0:T(8,128)(2,1)} %bitcast.8), kind=kLoop, calls=%fused_computation.6 | loop fusion | flops 64 | bytes 384 | tf_op jit(solution)/shard_map/convert_element_type | solution.py:984
  52.2 0.2 convert_reduce_fusion
  52.3 0.8 convert_reduce_fusion.1
  53.2 0.2 fusion.2
  53.3 0.1 select_reduce_fusion
  53.5 0.7 concatenate.11.table
  54.1 15.5 %attention_forward.1 = (bf16[2,64,64,128]{3,2,1,0:T(8,128)(2,1)}, bf16[2,64,64,128]{3,2,1,0:T(8,128)(2,1)}, f32[2,2,256,128]{3,2,1,0:T(8,128)}, f32[2,2,256,128]{3,2,1,0:T(8,128)}) custom-call(s32[136]{0:T(256)} %concatenate.11.table, bf16[64,2,144,128]{3,2,1,0:T(8,128)(2,1)} %bitcast.9, bf16[2,128,512]{2,1,0:T(8,128)(2,1)} %get-tuple-element.30.q), custom_call_target="tpu_custom_call" | custom-call | tf_op jit(solution)/shard_map/attention_forward/pallas_call | solution.py:666
  69.6 4.9 %swap_partials.1 = (f32[2,2,256,128]{3,2,1,0:T(8,128)}, f32[2,2,256,128]{3,2,1,0:T(8,128)}) custom-call(f32[2,2,256,128]{3,2,1,0:T(8,128)} %get-tuple-element.34.a.o, f32[2,2,256,128]{3,2,1,0:T(8,128)} %get-tuple-element.35.b.lse), custom_call_target="tpu_custom_call" | custom-call | tf_op jit(solution)/shard_map/swap_partials/pallas_call | solution.py:516
  74.5 22.6 %attention_backward.1 = (bf16[128,512]{1,0:T(8,128)(2,1)}, bf16[64,2,128,128]{3,2,1,0:T(8,128)(2,1)}, f32[2,2,256,128]{3,2,1,0:T(8,128)}) custom-call(s32[136]{0:T(256)} %concatenate.11.table, bf16[2,64,64,128]{3,2,1,0:T(8,128)(2,1)} %get-tuple-element.31.ks, bf16[2,64,64,128]{3,2,1,0:T(8,128)(2,1)} %get-tuple-element.32.vs, ...), custom_call_target="tpu_custom_call" | custom-call | tf_op jit(solution)/shard_map/attention_backward/pallas_call | solution.py:797
  97.2 34.5 %scatter_kv.1 = (f32[2,2,256,128]{3,2,1,0:T(8,128)}, f32[2,2,128,128]{3,2,1,0:T(8,128)}) custom-call(bf16[2,4,4,2,2,128,128]{6,5,4,3,2,1,0:T(8,128)(2,1)} %bitcast.10, f32[2,2,256,128]{3,2,1,0:T(8,128)} %get-tuple-element.40.dq), custom_call_target="tpu_custom_call" | custom-call | tf_op jit(solution)/shard_map/scatter_kv/pallas_call | solution.py:443
  131.7 9.5 %token_grads.1 = (bf16[128,4096]{1,0:T(8,128)(2,1)}, bf16[2,4,4,2,32,768]{5,4,3,2,1,0:T(8,128)(2,1)}) custom-call(s32[136]{0:T(256)} %concatenate.11.table, f32[2,2,256,128]{3,2,1,0:T(8,128)} %get-tuple-element.41.dq, f32[2,2,128,128]{3,2,1,0:T(8,128)} %get-tuple-element.42.dkv, f32[2,2,128,128]{3,2,1,0:T(8,128)} %get-tuple-element.43.tables, ...), custom_call_target="tpu_custom_call" | custom-call | tf_op jit(solution)/shard_map/token_grads/pallas_call | solution.py:877
  141.2 27.7 %scatter_weights.1 = f32[32,768]{1,0:T(8,128)} custom-call(bf16[2,4,4,2,32,768]{5,4,3,2,1,0:T(8,128)(2,1)} %get-tuple-element.46.part), custom_call_target="tpu_custom_call" | custom-call | tf_op jit(solution)/shard_map/scatter_weights/pallas_call | solution.py:487
  168.9 1.3 fusion.3
  170.2 1.5 slice.21
  (1 shorter events, 0.0 us)
